TPU v7x, 32 devices: a whole 2x2x4 slice. The times are simulated.
32 devices in a mesh: fs: 4 (over z), pp: 2 (over y), ep: 4 (over x, core).
Axes of the slice: x: 2, y: 2, z: 4, core: 2. Of those that a mesh axis runs over, the one named last changes fastest.
Arguments:
- w_gate: bfloat16 [2, 96, 1024, 512], P('pp', 'ep', None, 'fs')
- w_up: bfloat16 [2, 96, 1024, 512], P('pp', 'ep', None, 'fs')
- w_down: bfloat16 [2, 96, 512, 1024], P('pp', 'ep', 'fs')
- hot_ids: int32 [6], replicated
Outputs:
- output 1: bfloat16 [2, 96, 1024, 1024], P(None, ('pp', 'ep', 'fs'))
- output 2: bfloat16 [2, 96, 512, 1024], P(None, ('pp', 'ep', 'fs'))
- output 3: bfloat16 [2, 6, 1024, 1024], replicated
- output 4: bfloat16 [2, 6, 512, 1024], replicated
All inputs are finite; a program needn't handle non-finite values.
Results may differ from a plain program's by a relative error of at most 0.001.
Values are sent between devices in bfloat16 or wider.
A program may use at most 1 GiB of HBM per device.

v0:
```python
import jax
import jax.numpy as jnp
from jax import lax
from jax.sharding import PartitionSpec as P


def solution(mesh):
    fs_size = mesh.shape["fs"]
    pp_size = mesh.shape["pp"]
    ep_size = mesh.shape["ep"]
    perm_pairs = [(stage_idx * ep_size + col_idx, col_idx * pp_size + stage_idx) for stage_idx in range(pp_size) for col_idx in range(ep_size)]
    in_spec = P("pp", "ep", None, "fs")
    down_spec = P("pp", "ep", "fs", None)
    home_spec = P(None, ("pp", "ep", "fs"), None, None)

    def regroup(shard_in, f_axis):
        lay_local = shard_in.shape[0]
        exp_local = shard_in.shape[1]
        per_dev = exp_local // (fs_size * pp_size)
        split_view = shard_in.reshape((lay_local, pp_size, fs_size, per_dev) + shard_in.shape[2:])
        moved_blk = lax.all_to_all(split_view, "fs", 2, f_axis + 2, tiled=True)
        moved_blk = lax.all_to_all(moved_blk, "pp", 1, 0, tiled=True)
        moved_blk = lax.ppermute(moved_blk, ("pp", "ep"), perm_pairs)
        return moved_blk.reshape((lay_local * pp_size, per_dev) + moved_blk.shape[4:])

    def hot_pick(shard_in, hot_ids, f_axis):
        exp_local = shard_in.shape[1]
        base_id = lax.axis_index("ep") * exp_local
        offset = hot_ids - base_id
        is_held = (offset >= 0) & (offset < exp_local)
        picked = jnp.take(shard_in, jnp.clip(offset, 0, exp_local - 1), axis=1)
        picked = jnp.where(is_held[None, :, None, None], picked, jnp.zeros((), picked.dtype))
        picked = lax.psum(picked, "ep")
        picked = lax.all_gather(picked, "pp", axis=0, tiled=True)
        return lax.all_gather(picked, "fs", axis=f_axis, tiled=True)

    def device_body(w_gate, w_up, w_down, hot_ids):
        gate_home = regroup(w_gate, 3)
        up_home = regroup(w_up, 3)
        down_home = regroup(w_down, 2)
        gate_up = jnp.concatenate([gate_home, up_home], axis=-1)
        hot_gate_up = jnp.concatenate([hot_pick(w_gate, hot_ids, 3), hot_pick(w_up, hot_ids, 3)], axis=-1)
        hot_down = hot_pick(w_down, hot_ids, 2)
        return gate_up, down_home, hot_gate_up, hot_down

    return jax.shard_map(device_body, mesh=mesh, in_specs=(in_spec, in_spec, down_spec, P()), out_specs=(home_spec, home_spec, P(), P()), check_vma=False)
```

profile of v0, /device:TPU:28, one launch (start us, length us, event | category | flops | bytes accessed | tf_op | source)
XLA Modules:
  0.0 1439.0 jit_solution(18370931117439468374)
XLA Ops:
  24.6 94.9 %all-reduce.3.cloned.1.call-done = (bf16[1,6,1024,128]{3,2,1,0:T(8,128)(2,1)}, bf16[1,6,1024,128]{3,2,1,0:T(8,128)(2,1)}, bf16[1,6,128,1024]{3,2,1,0:T(8,128)(2,1)}) async-done(((bf16[1,6,1024,128]{3,2,1,0:T(8,128)(2,1)}, bf16[1,6,1024,128]{3,2,1,0:T(8,128)(2,1)}, bf16[1,6,128,1024]{3,2,1,0:T(8,128)(2,1)}), (bf16[1,6,1024,128]{3,2,1,0:T(8,128)(2,1)}, bf16[1,6,1024,128]{3,2,1,0:T(8,128)(2,1)}, ...) | async-done | bytes 4718608 | tf_op jit(solution)/shard_map/psum | solution.py:33
  120.9 44.4 %all-gather.15.cloned.1.call-done = bf16[2,6,128,1024]{3,2,1,0:T(8,128)(2,1)} async-done(((bf16[1,6,128,1024]{3,2,1,0:T(8,128)(2,1)}), bf16[2,6,128,1024]{3,2,1,0:T(8,128)(2,1)}) %all-gather.15.cloned.1.call-update) | async-done | bytes 3145744 | tf_op jit(solution)/shard_map/all_gather | solution.py:34
  165.3 6.1 copy.14
  176.9 34.9 %all-gather.11.cloned.1.call-done = bf16[2,6,1024,128]{3,2,1,0:T(8,128)(2,1)} async-done(((bf16[1,6,1024,128]{3,2,1,0:T(8,128)(2,1)}), bf16[2,6,1024,128]{3,2,1,0:T(8,128)(2,1)}) %all-gather.11.cloned.1.call-update) | async-done | bytes 3145744 | tf_op jit(solution)/shard_map/all_gather | solution.py:34
  217.9 196.9 %all-to-all-done.2 = bf16[1,2,4,3,1024,128]{5,4,3,1,0,2:T(8,128)(2,1)} async-done(((bf16[1,2,4,3,1024,128]{5,4,3,1,0,2:T(8,128)(2,1)}), bf16[1,2,4,3,1024,128]{5,4,3,1,0,2:T(8,128)(2,1)}, u32[]{:S(2)}, u32[]{:S(2)}) %all-to-all-start.2) | async-done | bytes 6291488 | tf_op jit(solution)/shard_map/all_to_all | solution.py:21
  420.5 6.6 copy.17
  427.0 223.0 %all-to-all-done = bf16[1,2,4,3,1024,128]{5,4,3,1,0,2:T(8,128)(2,1)} async-done(((bf16[1,2,4,3,1024,128]{5,4,3,1,0,2:T(8,128)(2,1)}), bf16[1,2,4,3,1024,128]{5,4,3,1,0,2:T(8,128)(2,1)}, u32[]{:S(2)}, u32[]{:S(2)}) %all-to-all-start) | async-done | bytes 6291488 | tf_op jit(solution)/shard_map/all_to_all | solution.py:21
  650.0 7.6 all-to-all-start.4
  658.4 8.6 copy.15
  667.0 8.6 copy.16
  675.6 285.2 %all-to-all-done.4 = bf16[1,2,4,3,128,1024]{5,4,3,1,0,2:T(8,128)(2,1)} async-done(((bf16[1,2,4,3,128,1024]{5,4,3,1,0,2:T(8,128)(2,1)}), bf16[1,2,4,3,128,1024]{5,4,3,1,0,2:T(8,128)(2,1)}, u32[]{:S(2)}, u32[]{:S(2)}) %all-to-all-start.4) | async-done | bytes 6291488 | tf_op jit(solution)/shard_map/all_to_all | solution.py:21
  960.8 8.2 all-to-all-start.3
  969.0 6.6 copy.18
  975.6 59.4 %all-to-all-done.3 = bf16[1,2,1,3,1024,512]{5,4,3,2,0,1:T(8,128)(2,1)} async-done(((bf16[1,2,1,3,1024,512]{5,4,3,2,0,1:T(8,128)(2,1)}), bf16[1,2,1,3,1024,512]{5,4,3,2,0,1:T(8,128)(2,1)}, u32[]{:S(2)}, u32[]{:S(2)}) %all-to-all-start.3) | async-done | bytes 6291488 | tf_op jit(solution)/shard_map/all_to_all | solution.py:22
  1035.0 8.0 all-to-all-start.5
  1043.0 8.6 copy.12
  1051.7 8.6 copy.13
  1060.3 48.0 %all-to-all-done.5 = bf16[1,2,1,3,512,1024]{5,4,3,2,0,1:T(8,128)(2,1)} async-done(((bf16[1,2,1,3,512,1024]{5,4,3,2,0,1:T(8,128)(2,1)}), bf16[1,2,1,3,512,1024]{5,4,3,2,0,1:T(8,128)(2,1)}, u32[]{:S(2)}, u32[]{:S(2)}) %all-to-all-start.5) | async-done | bytes 6291488 | tf_op jit(solution)/shard_map/all_to_all | solution.py:22
  1108.3 8.0 all-to-all-start.1
  1120.5 195.1 %all-to-all-done.1 = bf16[1,2,1,3,1024,512]{5,4,3,2,0,1:T(8,128)(2,1)} async-done(((bf16[1,2,1,3,1024,512]{5,4,3,2,0,1:T(8,128)(2,1)}), bf16[1,2,1,3,1024,512]{5,4,3,2,0,1:T(8,128)(2,1)}, u32[]{:S(2)}, u32[]{:S(2)}) %all-to-all-start.1) | async-done | bytes 6291488 | tf_op jit(solution)/shard_map/all_to_all | solution.py:22
  1317.6 71.8 %collective-permute-done = bf16[2,1,1,3,1024,512]{5,4,3,0,2,1:T(8,128)(2,1)S(1)} collective-permute-done((bf16[2,1,1,3,1024,512]{5,4,3,0,2,1:T(8,128)(2,1)}, bf16[2,1,1,3,1024,512]{5,4,3,0,2,1:T(8,128)(2,1)S(1)}, u32[]{:S(2)}, u32[]{:S(2)}) %collective-permute-start) | collective-permute-done | bytes 6291488 | tf_op jit(solution)/shard_map/ppermute | solution.py:23
  1389.4 8.4 pad_maximum_fusion.1
  1397.8 20.9 %pad_maximum_fusion = bf16[2,6,1024,1024]{3,2,1,0:T(8,128)(2,1)} fusion(bf16[2,6,1024,512]{3,2,1,0:T(8,128)(2,1)} %all-gather.13.cloned.1.call-done, bf16[2,6,1024,512]{3,2,1,0:T(8,128)(2,1)} %all-gather.9.cloned.1.call-done), kind=kLoop, calls=%fused_computation.3 | loop fusion | flops 50331648 | bytes 50331648 | tf_op jit(solution)/shard_map/concatenate | solution.py:42
  1418.7 7.5 copy.25
  (36 shorter events, 48.8 us)
Async XLA Ops:
  7.2 112.4 %all-reduce.3.cloned.1.call-start = ((), (), s32[]{:S(2)}) async-start(), calls=%async_computation.12 | async-start | bytes 9437184 | tf_op jit(solution)/shard_map/psum | solution.py:33
  24.6 140.7 %all-gather.15.cloned.1.call-start = ((), (), s32[]{:S(2)}) async-start(), calls=%async_computation.10 | async-start | bytes 4718592 | tf_op jit(solution)/shard_map/all_gather | solution.py:34
  119.6 92.3 %all-gather.11.cloned.1.call-start = ((), (), s32[]{:S(2)}) async-start(), calls=%async_computation.8 | async-start | bytes 4718592 | tf_op jit(solution)/shard_map/all_gather | solution.py:34
  120.3 537.4 %all-gather.7.cloned.1.call-start = ((), (), s32[]{:S(2)}) async-start(), calls=%async_computation.6 | async-start | bytes 4718592 | tf_op jit(solution)/shard_map/all_gather | solution.py:34
  120.9 1277.0 %all-gather.17.cloned.1.call-start = ((), (), s32[]{:S(2)}) async-start(), calls=%async_computation.11 | async-start | bytes 15728640 | tf_op jit(solution)/shard_map/all_gather | solution.py:35
  171.4 243.4 %all-to-all-start.2 = ((bf16[1,2,4,3,1024,128]{5,4,3,1,0,2:T(8,128)(2,1)}), bf16[1,2,4,3,1024,128]{5,4,3,1,0,2:T(8,128)(2,1)}, u32[]{:S(2)}, u32[]{:S(2)}) async-start(bf16[1,2,4,3,1024,128]{5,4,3,1,0,2:T(8,128)(2,1)} %copy.14), calls=%async_computation.2 | async-start | bytes 12582912 | tf_op jit(solution)/shard_map/all_to_all | solution.py:21
  176.9 1220.9 %all-gather.13.cloned.1.call-start = ((), (), s32[]{:S(2)}) async-start(), calls=%async_computation.9 | async-start | bytes 15728640 | tf_op jit(solution)/shard_map/all_gather | solution.py:35
  414.8 235.2 %all-to-all-start = ((bf16[1,2,4,3,1024,128]{5,4,3,1,0,2:T(8,128)(2,1)}), bf16[1,2,4,3,1024,128]{5,4,3,1,0,2:T(8,128)(2,1)}, u32[]{:S(2)}, u32[]{:S(2)}) async-start(bf16[1,2,4,3,1024,128]{5,4,3,1,0,2:T(8,128)(2,1)} %copy.11), calls=%async_computation | async-start | bytes 12582912 | tf_op jit(solution)/shard_map/all_to_all | solution.py:21
  650.0 310.8 %all-to-all-start.4 = ((bf16[1,2,4,3,128,1024]{5,4,3,1,0,2:T(8,128)(2,1)}), bf16[1,2,4,3,128,1024]{5,4,3,1,0,2:T(8,128)(2,1)}, u32[]{:S(2)}, u32[]{:S(2)}) async-start(bf16[1,2,4,3,128,1024]{5,4,3,1,0,2:T(8,128)(2,1)} %copy.17), calls=%async_computation.4 | async-start | bytes 12582912 | tf_op jit(solution)/shard_map/all_to_all | solution.py:21
  657.7 740.2 %all-gather.9.cloned.1.call-start = ((), (), s32[]{:S(2)}) async-start(), calls=%async_computation.7 | async-start | bytes 15728640 | tf_op jit(solution)/shard_map/all_gather | solution.py:35
  960.8 74.2 %all-to-all-start.3 = ((bf16[1,2,1,3,1024,512]{5,4,3,2,0,1:T(8,128)(2,1)}), bf16[1,2,1,3,1024,512]{5,4,3,2,0,1:T(8,128)(2,1)}, u32[]{:S(2)}, u32[]{:S(2)}) async-start(bf16[1,2,1,3,1024,512]{5,4,3,2,0,1:T(8,128)(2,1)} %copy.16), calls=%async_computation.3 | async-start | bytes 12582912 | tf_op jit(solution)/shard_map/all_to_all | solution.py:22
  1035.0 73.3 %all-to-all-start.5 = ((bf16[1,2,1,3,512,1024]{5,4,3,2,0,1:T(8,128)(2,1)}), bf16[1,2,1,3,512,1024]{5,4,3,2,0,1:T(8,128)(2,1)}, u32[]{:S(2)}, u32[]{:S(2)}) async-start(bf16[1,2,1,3,512,1024]{5,4,3,2,0,1:T(8,128)(2,1)} %bitcast.41), calls=%async_computation.5 | async-start | bytes 12582912 | tf_op jit(solution)/shard_map/all_to_all | solution.py:22
  1108.3 207.3 %all-to-all-start.1 = ((bf16[1,2,1,3,1024,512]{5,4,3,2,0,1:T(8,128)(2,1)}), bf16[1,2,1,3,1024,512]{5,4,3,2,0,1:T(8,128)(2,1)}, u32[]{:S(2)}, u32[]{:S(2)}) async-start(bf16[1,2,1,3,1024,512]{5,4,3,2,0,1:T(8,128)(2,1)} %copy.13), calls=%async_computation.1 | async-start | bytes 12582912 | tf_op jit(solution)/shard_map/all_to_all | solution.py:22
  1116.3 201.2 %collective-permute-start.2 = (bf16[2,1,1,3,512,1024]{5,4,3,0,2,1:T(8,128)(2,1)}, bf16[2,1,1,3,512,1024]{5,4,3,0,2,1:T(8,128)(2,1)}, u32[]{:S(2)}, u32[]{:S(2)}) collective-permute-start(bf16[2,1,1,3,512,1024]{5,4,3,0,2,1:T(8,128)(2,1)} %bitcast.17), channel_id=1, source_target_pairs={{0,0},{1,2},{2,4},{3,6},{4,1},{5,3},{6,5},{7,7},{8,8},{9,10},{10,1... | collective-permute-start | bytes 18874376 | tf_op jit(solution)/shard_map/ppermute | solution.py:23
  1118.2 199.3 %collective-permute-start.1 = (bf16[2,1,1,3,1024,512]{5,4,3,0,2,1:T(8,128)(2,1)}, bf16[2,1,1,3,1024,512]{5,4,3,0,2,1:T(8,128)(2,1)}, u32[]{:S(2)}, u32[]{:S(2)}) collective-permute-start(bf16[2,1,1,3,1024,512]{5,4,3,0,2,1:T(8,128)(2,1)} %bitcast.10), channel_id=1, source_target_pairs={{0,0},{1,2},{2,4},{3,6},{4,1},{5,3},{6,5},{7,7},{8,8},{9,10},{10,1... | collective-permute-start | bytes 18874376 | tf_op jit(solution)/shard_map/ppermute | solution.py:23
  1315.6 73.8 %collective-permute-start = (bf16[2,1,1,3,1024,512]{5,4,3,0,2,1:T(8,128)(2,1)}, bf16[2,1,1,3,1024,512]{5,4,3,0,2,1:T(8,128)(2,1)S(1)}, u32[]{:S(2)}, u32[]{:S(2)}) collective-permute-start(bf16[2,1,1,3,1024,512]{5,4,3,0,2,1:T(8,128)(2,1)} %bitcast.4), channel_id=1, source_target_pairs={{0,0},{1,2},{2,4},{3,6},{4,1},{5,3},{6,5},{7,7},{8,8},{9,10},{10,1... | collective-permute-start | bytes 18874376 | tf_op jit(solution)/shard_map/ppermute | solution.py:23
  1418.7 8.7 copy-start
Sparse Core Ops, SparseCore 0:
  24.7 94.7 all-reduce.2
  121.1 44.1 all-gather.14
  166.9 44.9 all-gather.10
  213.2 44.9 all-gather.6
  259.6 383.9 all-gather.16
  645.1 350.8 all-gather.12
  997.5 217.9 all-gather.8
where the time goes:
time: 1450 us; the launch traced here: 1440 us
  waiting for transfers between devices  1260 us (87%)
  local copies, waits for them, and re-layouts  85 us (6%)
  starting transfers between devices  49.3 us (3%)
  other arithmetic  34.8 us (2%)
    all_to_all x3, waiting for transfers between devices, regroup(): moved_blk = lax.all_to_all(split_view, 'fs', 2, f_axis + 2, tiled=True)  705 us
    all_to_all x3, waiting for transfers between devices, regroup(): moved_blk = lax.all_to_all(moved_blk, 'pp', 1, 0, tiled=True)  303 us
    psum x1, waiting for transfers between devices, hot_pick(): picked = lax.psum(picked, 'ep')  94.9 us
    all_gather x3, waiting for transfers between devices, hot_pick(): picked = lax.all_gather(picked, 'pp', axis=0, tiled=True)  79.3 us
    ppermute x3, waiting for transfers between devices, regroup(): moved_blk = lax.ppermute(moved_blk, ('pp', 'ep'), perm_pairs)  71.8 us
    all_to_all x5, local copies, waits for them, and re-layouts, regroup(): moved_blk = lax.all_to_all(split_view, 'fs', 2, f_axis + 2, tiled=True)  41 us
  transfers between devices with their start and end apart: 16, of which 10 were waited for; matrix products, arithmetic and copies ran while one was open for 5% of the time, Pallas kernels for 0%

commit v1 on v0

v1 whole, which is shorter than its diff:
```python
import functools

import jax
import jax.numpy as jnp
from jax import lax
from jax.experimental import pallas as pl
from jax.experimental.pallas import tpu as pltpu
from jax.sharding import PartitionSpec as P

ANY = pl.BlockSpec(memory_space=pl.ANY)
MESH = pl.DeviceIdType.MESH
FS, PP, EP = 4, 2, 4
N_T = 3


def pick_body(off_ref, gate_in, up_in, down_in, gate_out, up_out, down_out):
    gate_out[...] = gate_in[0]
    up_out[...] = up_in[0]
    down_out[...] = down_in[0]


def pick(w_gate, w_up, w_down, offset):
    hot = offset.shape[0]
    d, f = w_gate.shape[2:]
    src = lambda a, b: pl.BlockSpec((1, 1, a, b), lambda h, off: (0, off[h], 0, 0))
    dst = lambda a, b: pl.BlockSpec((1, a, b), lambda h, off: (h, 0, 0))
    return pl.pallas_call(
        pick_body,
        out_shape=(
            jax.ShapeDtypeStruct((hot, d, f), w_gate.dtype),
            jax.ShapeDtypeStruct((hot, d, f), w_gate.dtype),
            jax.ShapeDtypeStruct((hot, f, d), w_gate.dtype),
        ),
        grid_spec=pltpu.PrefetchScalarGridSpec(
            num_scalar_prefetch=1,
            grid=(hot,),
            in_specs=[src(d, f), src(d, f), src(f, d)],
            out_specs=[dst(d, f), dst(d, f), dst(f, d)],
        ),
        name="pick",
    )(offset, w_gate, w_up, w_down)


def exchange_body(
    exp_per_ep, ids, gate, up, down, hot_g, hot_u, hot_d, w13, w2, hot13, hot2,
    cand_g, cand_u, cand_d, sel_g, sel_u, sel_d,
    main_s, main_r, rs_s, rs_r, loc, own, z_s, z_r, x_s, x_r, y_s, y_r, p_s, p_r, da_s, da_r, db_s, db_r, px_s, px_r, py_s, py_r, pa_s, pa_r, pb_s, pb_r,
):
    z, p, e = lax.axis_index("fs"), lax.axis_index("pp"), lax.axis_index("ep")
    x, c = e // 2, lax.rem(e, 2)
    width = gate.shape[3]
    hot = hot_g.shape[0]
    cut_g, cut_d = hot_g.shape[1] // EP, hot_d.shape[1] // EP
    full = gate.shape[3] * FS

    def remote(s, d, ss, rs, to):
        return pltpu.make_async_remote_copy(s, d, ss, rs, device_id=to, device_id_type=MESH)

    def landed(d, rs):
        pltpu.make_async_copy(d, d, rs).wait()

    def home(lay, zz):
        col = pl.multiple_of(zz * width, width)
        return (
            w13.at[lay, :, :, pl.ds(col, width)],
            w13.at[lay, :, :, pl.ds(pl.multiple_of(full + col, width), width)],
            w2.at[lay, :, pl.ds(col, width), :],
        )

    def main_to(zz, b):
        return (zz, x, lax.rem(2 * e + b, EP))

    def main_is_self(zz, b):
        return jnp.logical_and(jnp.logical_and(x == p, lax.rem(2 * e + b, EP) == e), zz == z)

    def main_copies(zz, b):
        k = b * FS + zz
        src = pl.ds(3 * k, 3)
        return [(a.at[0, src], d, k * N_T + t) for t, (a, d) in enumerate(zip((gate, up, down), home(p, z)))]

    def main_start(zz, b):
        mine = main_is_self(zz, b)

        @pl.when(jnp.logical_not(mine))
        def _():
            for s, d, i in main_copies(zz, b):
                remote(s, d, main_s.at[i], main_r.at[(p * FS + z) * N_T + lax.rem(i, N_T)], main_to(zz, b)).start()

        @pl.when(mine)
        def _():
            for t, (s, d, i) in enumerate(main_copies(zz, b)):
                pltpu.make_async_copy(s, d, loc.at[t]).start()

    def main_sent(zz, b):
        mine = main_is_self(zz, b)

        @pl.when(jnp.logical_not(mine))
        def _():
            for s, d, i in main_copies(zz, b):
                remote(s, d, main_s.at[i], main_s.at[i], main_to(zz, b)).wait_send()

        @pl.when(mine)
        def _():
            for t, (s, d, i) in enumerate(main_copies(zz, b)):
                pltpu.make_async_copy(s, d, loc.at[t]).wait()

    def main_landed(ys, zs):
        mine = jnp.logical_and(jnp.logical_and(2 * p + x == e, p == ys), z == zs)

        @pl.when(jnp.logical_not(mine))
        def _():
            for t, d in enumerate(home(ys, zs)):
                landed(d, main_r.at[(ys * FS + zs) * N_T + t])

    def piece(yy, q, zz, lo=0, hi=hot):
        col = pl.multiple_of(zz * width, width)
        rows = pl.ds(pl.multiple_of(q * cut_g, cut_g), cut_g)
        slots = pl.ds(lo, hi - lo)
        return (
            hot13.at[yy, slots, rows, pl.ds(col, width)],
            hot13.at[yy, slots, rows, pl.ds(pl.multiple_of(full + col, width), width)],
            hot2.at[yy, slots, pl.ds(pl.multiple_of(col + q * cut_d, cut_d), cut_d), :],
        )

    half = hot // 2
    q_x, q_p = 2 * (1 - x) + c, 2 * x + (1 - c)
    to_x, to_y, to_p = (z, p, q_x), (z, 1 - p, e), (z, p, q_p)

    def send(src, dst, ss, rs, i, to):
        for t in range(N_T):
            remote(src[t], dst[t], ss.at[i * N_T + t], rs.at[i * N_T + t], to).start()

    def sent(src, ss, i, to):
        for t in range(N_T):
            remote(src[t], src[t], ss.at[i * N_T + t], ss.at[i * N_T + t], to).wait_send()

    def arrived(dst, rs, i):
        for t in range(N_T):
            landed(dst[t], rs.at[i * N_T + t])

    def part(q):
        return (
            hot_g.at[:, pl.ds(pl.multiple_of(q * cut_g, cut_g), cut_g), :],
            hot_u.at[:, pl.ds(pl.multiple_of(q * cut_g, cut_g), cut_g), :],
            hot_d.at[:, pl.ds(pl.multiple_of(q * cut_d, cut_d), cut_d), :],
        )

    def cand(q):
        return cand_g.at[q], cand_u.at[q], cand_d.at[q]

    for k in range(1, EP):
        q = lax.rem(e + k, EP)
        for t in range(N_T):
            remote(part(q)[t], cand(e)[t], rs_s.at[k * N_T + t], rs_r.at[k * N_T + t], (z, p, q)).start()
    for t in range(N_T):
        pltpu.make_async_copy(part(e)[t], cand(e)[t], own.at[t]).start()

    order = [(kk, b) for kk in (2, 1, 3, 0) for b in range(2)]
    for kk, b in order:
        main_start(lax.rem(z + kk, FS), b)

    for t in range(N_T):
        pltpu.make_async_copy(part(e)[t], cand(e)[t], own.at[t]).wait()
    for k in range(1, EP):
        q = lax.rem(e + EP - k, EP)
        for t in range(N_T):
            landed(cand(q)[t], rs_r.at[k * N_T + t])

    for h in range(hot):
        holder = ids[h] // exp_per_ep
        sel_g[h] = cand_g[holder, h]
        sel_u[h] = cand_u[holder, h]
        sel_d[h] = cand_d[holder, h]
    sel = (sel_g, sel_u, sel_d)

    def broadcast(src, zz, k):
        dst = piece(p, e, zz)
        send(src, dst, x_s, x_r, k, to_x)
        send(src, dst, y_s, y_r, k, to_y)
        send(src, dst, p_s, p_r, k, to_p)

    mine = piece(p, e, z)
    UP, DOWN = 0, 1

    @pl.when(z < FS - 1)
    def _():
        send(sel, mine, z_s, z_r, UP * FS + 1, (z + 1, p, e))

    @pl.when(z > 0)
    def _():
        send(sel, mine, z_s, z_r, DOWN * FS + 1, (z - 1, p, e))

    broadcast(sel, z, z)
    for t in range(N_T):
        pltpu.make_async_copy(sel[t], mine[t], own.at[t]).start()

    def z_step(k):
        @pl.when(z - k >= 0)
        def _():
            src = piece(p, e, z - k)
            arrived(src, z_r, UP * FS + k)

            @pl.when(z < FS - 1)
            def _():
                send(src, src, z_s, z_r, UP * FS + k + 1, (z + 1, p, e))

            broadcast(src, z - k, z - k)

        @pl.when(z + k < FS)
        def _():
            src = piece(p, e, z + k)
            arrived(src, z_r, DOWN * FS + k)

            @pl.when(z > 0)
            def _():
                send(src, src, z_s, z_r, DOWN * FS + k + 1, (z - 1, p, e))

            broadcast(src, z + k, z + k)

    def plane_step(zz):
        from_x = piece(p, q_x, zz)
        arrived(from_x, x_r, zz)
        a = piece(p, q_x, zz, 0, half)
        send(a, a, da_s, da_r, zz, to_y)
        send(from_x, from_x, px_s, px_r, zz, to_p)
        from_y = piece(1 - p, e, zz)
        arrived(from_y, y_r, zz)
        b = piece(1 - p, e, zz, half, hot)
        send(b, b, db_s, db_r, zz, to_x)
        send(from_y, from_y, py_s, py_r, zz, to_p)

    def diagonal_step(zz):
        a = piece(1 - p, q_x, zz, 0, half)
        arrived(a, da_r, zz)
        send(a, a, pa_s, pa_r, zz, to_p)
        b = piece(1 - p, q_x, zz, half, hot)
        arrived(b, db_r, zz)
        send(b, b, pb_s, pb_r, zz, to_p)

    for k in range(1, FS):
        z_step(k)
    for k in range(FS):
        plane_step(lax.rem(z + k, FS))
    for k in range(FS):
        diagonal_step(lax.rem(z + k, FS))

    for t in range(N_T):
        pltpu.make_async_copy(sel[t], mine[t], own.at[t]).wait()
    for k in range(1, EP):
        q = lax.rem(e + k, EP)
        for t in range(N_T):
            remote(part(q)[t], cand(e)[t], rs_s.at[k * N_T + t], rs_s.at[k * N_T + t], (z, p, q)).wait_send()
    for k in range(1, FS):
        @pl.when(jnp.logical_and(z - k + 1 >= 0, z < FS - 1))
        def _():
            sent(mine, z_s, UP * FS + k, (z + 1, p, e))

        @pl.when(jnp.logical_and(z + k - 1 < FS, z > 0))
        def _():
            sent(mine, z_s, DOWN * FS + k, (z - 1, p, e))
    for zz in range(FS):
        src = piece(p, e, zz)
        sent(src, x_s, zz, to_x)
        sent(src, y_s, zz, to_y)
        sent(src, p_s, zz, to_p)
        sent(src, px_s, zz, to_p)
        sent(src, py_s, zz, to_p)
        a = piece(p, q_x, zz, 0, half)
        sent(a, da_s, zz, to_y)
        sent(a, db_s, zz, to_x)
        sent(a, pa_s, zz, to_p)
        sent(a, pb_s, zz, to_p)
        q_px = 2 * (1 - x) + (1 - c)
        arrived(piece(p, q_p, zz), p_r, zz)
        arrived(piece(p, q_px, zz), px_r, zz)
        arrived(piece(1 - p, q_p, zz), py_r, zz)
        arrived(piece(1 - p, q_px, zz, 0, half), pa_r, zz)
        arrived(piece(1 - p, q_px, zz, half, hot), pb_r, zz)
    for kk, b in order:
        main_sent(lax.rem(z + kk, FS), b)
    for ys in range(PP):
        for zs in range(FS):
            main_landed(ys, zs)


def exchange(ids, w_gate, w_up, w_down, hot_g, hot_u, hot_d):
    dt = w_gate.dtype
    exp_local, d, f = w_gate.shape[1:]
    hot = hot_g.shape[0]
    per_dev = exp_local // (FS * PP)
    full = f * FS
    dma = lambda n: pltpu.SemaphoreType.DMA((n,))
    quarter = [(hot, d // EP, f), (hot, d // EP, f), (hot, f // EP, d)]
    four = lambda: [dma(FS * N_T), dma(FS * N_T)]
    return pl.pallas_call(
        functools.partial(exchange_body, exp_local),
        out_shape=(
            jax.ShapeDtypeStruct((PP, per_dev, d, 2 * full), dt),
            jax.ShapeDtypeStruct((PP, per_dev, full, d), dt),
            jax.ShapeDtypeStruct((PP, hot, d, 2 * full), dt),
            jax.ShapeDtypeStruct((PP, hot, full, d), dt),
        ),
        in_specs=[pl.BlockSpec(memory_space=pltpu.SMEM)] + [ANY] * 6,
        out_specs=(ANY,) * 4,
        scratch_shapes=[pltpu.VMEM((EP,) + s, dt) for s in quarter]
        + [pltpu.VMEM(s, dt) for s in quarter]
        + [dma(FS * PP * N_T), dma(FS * PP * N_T), dma(EP * N_T), dma(EP * N_T), dma(N_T), dma(N_T)]
        + [dma(2 * FS * N_T), dma(2 * FS * N_T)]
        + four() * 9,
        compiler_params=pltpu.CompilerParams(has_side_effects=True),
        name="exchange",
    )(ids, w_gate, w_up, w_down, hot_g, hot_u, hot_d)


def solution(mesh):
    in_spec = P("pp", "ep", None, "fs")
    down_spec = P("pp", "ep", "fs", None)
    home_spec = P(None, ("pp", "ep", "fs"), None, None)

    def device_body(w_gate, w_up, w_down, hot_ids):
        exp_local = w_gate.shape[1]
        offset = jnp.clip(hot_ids - lax.axis_index("ep") * exp_local, 0, exp_local - 1)
        picked = pick(w_gate, w_up, w_down, offset)
        return exchange(hot_ids, w_gate, w_up, w_down, *picked)

    return jax.shard_map(
        device_body,
        mesh=mesh,
        in_specs=(in_spec, in_spec, down_spec, P()),
        out_specs=(home_spec, home_spec, P(), P()),
        check_vma=False,
    )
```

time: 1450 us -> 628 us (0.43)
  the two profiles are of different devices: /device:TPU:28 before, /device:TPU:0 now
where the time goes in v1:
time: 628 us; the launch traced here: 627 us
  Pallas kernels  583 us (93%)
  local copies, waits for them, and re-layouts  41.3 us (7%)
    pallas_call x1, Pallas kernels, exchange(): pl.pallas_call(functools.partial(exchange_body, exp_local), out_shape=(ja...  577 us
    unnamed x12, local copies, waits for them, and re-layouts  41.3 us

profile of v1, /device:TPU:0, one launch (start us, length us, event | category | flops | bytes accessed | tf_op | source)
XLA Modules:
  0.0 626.6 jit_solution(15606368674050554385)
XLA Ops:
  0.6 1.2 subtract_clamp_fusion.off_ref
  1.8 6.6 %pick.1 = (bf16[6,1024,128]{2,1,0:T(8,128)(2,1)}, bf16[6,1024,128]{2,1,0:T(8,128)(2,1)}, bf16[6,128,1024]{2,1,0:T(8,128)(2,1)}) custom-call(s32[6]{0:T(128)} %subtract_clamp_fusion.off_ref, bf16[1,24,1024,128]{3,2,1,0:T(8,128)(2,1)} %gate.1, bf16[1,24,1024,128]{3,2,1,0:T(8,128)(2,1)} %up.1, bf16[1,24,128,1024]{3,2,1,0:T(8,128)(2,1)} %down.1), custom_call_target="tpu_custom_call" | custom-call | tf_op jit(solution)/shard_map/pick/pallas_call | solution.py:27
  8.4 576.9 %exchange.1 = (bf16[2,3,1024,1024]{3,2,1,0:T(8,128)(2,1)}, bf16[2,3,512,1024]{3,2,1,0:T(8,128)(2,1)}, bf16[2,6,1024,1024]{3,2,1,0:T(8,128)(2,1)}, bf16[2,6,512,1024]{3,2,1,0:T(8,128)(2,1)}) custom-call(s32[6]{0:T(128)} %ids.1, bf16[1,24,1024,128]{3,2,1,0:T(8,128)(2,1)} %gate.1, bf16[1,24,1024,128]{3,2,1,0:T(8,128)(2,1)} %up.1, ...), custom_call_target="tpu_custom_call" | custom-call | tf_op jit(solution)/shard_map/exchange/pallas_call | solution.py:295
  585.3 0.0 copy-start
  585.3 11.0 %copy.12 = bf16[2,3,1024,1024]{3,2,1,0:T(8,128)(2,1)} copy(bf16[2,3,1024,1024]{3,2,1,0:T(8,128)(2,1)} %get-tuple-element.14) | data formatting | bytes 25165824
  596.3 0.0 copy-done
  596.3 0.0 slice-start
  596.3 3.2 copy.13
  599.5 0.0 slice-start.1
  599.5 0.0 slice-start.2
  599.5 22.2 %copy.14 = bf16[2,6,1024,1024]{3,2,1,0:T(8,128)(2,1)} copy(bf16[2,6,1024,1024]{3,2,1,0:T(8,128)(2,1)} %get-tuple-element.16) | data formatting | bytes 50331648
  621.8 0.0 slice-done
  621.8 0.0 slice-done.1
  621.8 0.0 slice-done.2
  621.8 4.8 copy.15
  (1 shorter events, 0.0 us)
Async XLA Ops:
  585.3 11.1 %copy-start = (bf16[2,3,512,1024]{3,2,1,0:T(8,128)(2,1)S(1)}, bf16[2,3,512,1024]{3,2,1,0:T(8,128)(2,1)}, u32[]{:S(2)}) copy-start(bf16[2,3,512,1024]{3,2,1,0:T(8,128)(2,1)} %get-tuple-element.15) | copy-start | bytes 18874372
  596.3 25.4 %slice-start = ((s8[12582912]{0:T(1024)(128)(4,1)}), s8[4194304]{0:T(1024)(128)(4,1)S(1)}, s32[]{:S(2)}) async-start(s8[12582912]{0:T(1024)(128)(4,1)} %bitcast), calls=%async_computation | async-start | bytes 8388608
  599.5 22.2 %slice-start.1 = ((s8[12582912]{0:T(1024)(128)(4,1)}), s8[4194304]{0:T(1024)(128)(4,1)S(1)}, s32[]{:S(2)}) async-start(s8[12582912]{0:T(1024)(128)(4,1)} %bitcast), calls=%async_computation.1 | async-start | bytes 8388608
  599.5 22.2 %slice-start.2 = ((s8[12582912]{0:T(1024)(128)(4,1)}), s8[4194304]{0:T(1024)(128)(4,1)S(1)}, s32[]{:S(2)}) async-start(s8[12582912]{0:T(1024)(128)(4,1)} %bitcast), calls=%async_computation.2 | async-start | bytes 8388608

commit v2 on v1

--- a/solution.py
+++ b/solution.py
@@ -11,6 +11,9 @@
 MESH = pl.DeviceIdType.MESH
 FS, PP, EP = 4, 2, 4
 N_T = 3
+LATE = 2
+ORDER = [(kk, b, t) for t in range(N_T) for b in range(2) for kk in (1, 3, 2, 0) if (kk, b, t) != (LATE, 1, 2)]
+BATCH = (8, 0, 0, 0, 0)
 
 
 def pick_body(off_ref, gate_in, up_in, down_in, gate_out, up_out, down_out):
@@ -42,7 +45,7 @@
 
 
 def exchange_body(
-    exp_per_ep, ids, gate, up, down, hot_g, hot_u, hot_d, w13, w2, hot13, hot2,
+    exp_per_ep, ids, gate, up, down, hot_g, hot_u, hot_d, w13, w2, hot13, hot2, late,
     cand_g, cand_u, cand_d, sel_g, sel_u, sel_d,
     main_s, main_r, rs_s, rs_r, loc, own, z_s, z_r, x_s, x_r, y_s, y_r, p_s, p_r, da_s, da_r, db_s, db_r, px_s, px_r, py_s, py_r, pa_s, pa_r, pb_s, pb_r,
 ):
@@ -73,43 +76,53 @@
     def main_is_self(zz, b):
         return jnp.logical_and(jnp.logical_and(x == p, lax.rem(2 * e + b, EP) == e), zz == z)
 
-    def main_copies(zz, b):
+    def main_copy(zz, b, t):
         k = b * FS + zz
-        src = pl.ds(3 * k, 3)
-        return [(a.at[0, src], d, k * N_T + t) for t, (a, d) in enumerate(zip((gate, up, down), home(p, z)))]
-
-    def main_start(zz, b):
+        return (gate, up, down)[t].at[0, pl.ds(3 * k, 3)], home(p, z)[t], k * N_T + t
+
+    def main_start(zz, b, t):
         mine = main_is_self(zz, b)
+        s, d, i = main_copy(zz, b, t)
 
         @pl.when(jnp.logical_not(mine))
         def _():
-            for s, d, i in main_copies(zz, b):
-                remote(s, d, main_s.at[i], main_r.at[(p * FS + z) * N_T + lax.rem(i, N_T)], main_to(zz, b)).start()
+            remote(s, d, main_s.at[i], main_r.at[(p * FS + z) * N_T + t], main_to(zz, b)).start()
 
         @pl.when(mine)
         def _():
-            for t, (s, d, i) in enumerate(main_copies(zz, b)):
-                pltpu.make_async_copy(s, d, loc.at[t]).start()
-
-    def main_sent(zz, b):
+            pltpu.make_async_copy(s, d, loc.at[t]).start()
+
+    def main_sent(zz, b, t):
         mine = main_is_self(zz, b)
+        s, d, i = main_copy(zz, b, t)
 
         @pl.when(jnp.logical_not(mine))
         def _():
-            for s, d, i in main_copies(zz, b):
-                remote(s, d, main_s.at[i], main_s.at[i], main_to(zz, b)).wait_send()
+            remote(s, d, main_s.at[i], main_s.at[i], main_to(zz, b)).wait_send()
 
         @pl.when(mine)
         def _():
-            for t, (s, d, i) in enumerate(main_copies(zz, b)):
-                pltpu.make_async_copy(s, d, loc.at[t]).wait()
+            pltpu.make_async_copy(s, d, loc.at[t]).wait()
+
+    queue = [(lax.rem(z + kk, FS), 1 - p if (kk, t) == (LATE, 2) else b, t) for kk, b, t in ORDER]
+    late_src = down.at[0, pl.ds(3 * (p * FS + lax.rem(z + LATE, FS)), 3)]
+    pltpu.make_async_copy(late_src, late, loc.at[N_T]).start()
+    started = []
+
+    def main_next(n):
+        for item in queue[len(started) : len(started) + n]:
+            main_start(*item)
+            started.append(item)
 
     def main_landed(ys, zs):
         mine = jnp.logical_and(jnp.logical_and(2 * p + x == e, p == ys), z == zs)
 
-        @pl.when(jnp.logical_not(mine))
-        def _():
-            for t, d in enumerate(home(ys, zs)):
+        is_late = jnp.logical_and(ys == c, zs == lax.rem(z + LATE, FS))
+        for t, d in enumerate(home(ys, zs)):
+            skip = jnp.logical_or(mine, is_late) if t == 2 else mine
+
+            @pl.when(jnp.logical_not(skip))
+            def _():
                 landed(d, main_r.at[(ys * FS + zs) * N_T + t])
 
     def piece(yy, q, zz, lo=0, hi=hot):
@@ -155,9 +168,7 @@
     for t in range(N_T):
         pltpu.make_async_copy(part(e)[t], cand(e)[t], own.at[t]).start()
 
-    order = [(kk, b) for kk in (2, 1, 3, 0) for b in range(2)]
-    for kk, b in order:
-        main_start(lax.rem(z + kk, FS), b)
+    main_next(BATCH[0])
 
     for t in range(N_T):
         pltpu.make_async_copy(part(e)[t], cand(e)[t], own.at[t]).wait()
@@ -190,6 +201,7 @@
     def _():
         send(sel, mine, z_s, z_r, DOWN * FS + 1, (z - 1, p, e))
 
+    main_next(BATCH[1])
     broadcast(sel, z, z)
     for t in range(N_T):
         pltpu.make_async_copy(sel[t], mine[t], own.at[t]).start()
@@ -239,6 +251,8 @@
 
     for k in range(1, FS):
         z_step(k)
+        main_next(BATCH[1 + k])
+    main_next(len(queue))
     for k in range(FS):
         plane_step(lax.rem(z + k, FS))
     for k in range(FS):
@@ -276,8 +290,9 @@
         arrived(piece(1 - p, q_p, zz), py_r, zz)
         arrived(piece(1 - p, q_px, zz, 0, half), pa_r, zz)
         arrived(piece(1 - p, q_px, zz, half, hot), pb_r, zz)
-    for kk, b in order:
-        main_sent(lax.rem(z + kk, FS), b)
+    for item in queue:
+        main_sent(*item)
+    pltpu.make_async_copy(late_src, late, loc.at[N_T]).wait()
     for ys in range(PP):
         for zs in range(FS):
             main_landed(ys, zs)
@@ -299,12 +314,13 @@
             jax.ShapeDtypeStruct((PP, per_dev, full, d), dt),
             jax.ShapeDtypeStruct((PP, hot, d, 2 * full), dt),
             jax.ShapeDtypeStruct((PP, hot, full, d), dt),
+            jax.ShapeDtypeStruct((per_dev, f, d), dt),
         ),
         in_specs=[pl.BlockSpec(memory_space=pltpu.SMEM)] + [ANY] * 6,
-        out_specs=(ANY,) * 4,
+        out_specs=(ANY,) * 5,
         scratch_shapes=[pltpu.VMEM((EP,) + s, dt) for s in quarter]
         + [pltpu.VMEM(s, dt) for s in quarter]
-        + [dma(FS * PP * N_T), dma(FS * PP * N_T), dma(EP * N_T), dma(EP * N_T), dma(N_T), dma(N_T)]
+        + [dma(FS * PP * N_T), dma(FS * PP * N_T), dma(EP * N_T), dma(EP * N_T), dma(N_T + 1), dma(N_T)]
         + [dma(2 * FS * N_T), dma(2 * FS * N_T)]
         + four() * 9,
         compiler_params=pltpu.CompilerParams(has_side_effects=True),
@@ -312,6 +328,81 @@
     )(ids, w_gate, w_up, w_down, hot_g, hot_u, hot_d)
 
 
+def settle_body(n_slot, ahead, *refs):
+    n = (len(refs) - 3) // 2
+    src, dst, (buf, r_sem, w_sem) = refs[:n], refs[n : 2 * n], refs[2 * n :]
+    steps = [(a, i, j) for a in range(n) for i in range(src[a].shape[0]) for j in range(src[a].shape[1])]
+
+    def load(k):
+        a, i, j = steps[k]
+        return pltpu.make_async_copy(src[a].at[i, j], buf.at[k % n_slot, pl.ds(0, src[a].shape[2])], r_sem.at[k % n_slot])
+
+    def store(k):
+        a, i, j = steps[k]
+        return pltpu.make_async_copy(buf.at[k % n_slot, pl.ds(0, src[a].shape[2])], dst[a].at[i, j], w_sem.at[k % n_slot])
+
+    for k in range(min(ahead, len(steps))):
+        load(k).start()
+    for k in range(len(steps)):
+        load(k).wait()
+        store(k).start()
+        if k + ahead < len(steps):
+            if k + ahead >= n_slot:
+                store(k + ahead - n_slot).wait()
+            load(k + ahead).start()
+    for k in range(max(0, len(steps) - n_slot), len(steps)):
+        store(k).wait()
+
+
+def settle(*arrays):
+    n_slot, ahead = 12, 6
+    rows = max(a.shape[2] for a in arrays)
+    size = sum(a.size * a.dtype.itemsize for a in arrays)
+    return pl.pallas_call(
+        functools.partial(settle_body, n_slot, ahead),
+        out_shape=tuple(jax.ShapeDtypeStruct(a.shape, a.dtype) for a in arrays),
+        in_specs=[ANY] * len(arrays),
+        out_specs=(ANY,) * len(arrays),
+        scratch_shapes=[
+            pltpu.VMEM((n_slot, rows, arrays[0].shape[3]), arrays[0].dtype),
+            pltpu.SemaphoreType.DMA((n_slot,)),
+            pltpu.SemaphoreType.DMA((n_slot,)),
+        ],
+        cost_estimate=pl.CostEstimate(flops=size * 16, bytes_accessed=2 * size, transcendentals=0),
+        name="settle",
+    )(*arrays)
+
+
+def insert_body(at_ref, piece_in, whole_in, whole_out):
+    whole_out[0] = piece_in[...]
+
+
+def insert(whole, piece, lay, zz):
+    _, f, d = piece.shape
+    return pl.pallas_call(
+        insert_body,
+        out_shape=jax.ShapeDtypeStruct(whole.shape, whole.dtype),
+        grid_spec=pltpu.PrefetchScalarGridSpec(
+            num_scalar_prefetch=1,
+            grid=(piece.shape[0],),
+            in_specs=[pl.BlockSpec((1, f, d), lambda h, at: (h, 0, 0)), ANY],
+            out_specs=pl.BlockSpec((1, 1, f, d), lambda h, at: (at[0], h, at[1], 0)),
+        ),
+        input_output_aliases={2: 0},
+        name="insert",
+    )(jnp.stack([lay, zz]), piece, whole)
+
+
+def late_pairs():
+    flat = lambda z, p, e: (z * PP + p) * EP + e
+    return [
+        (flat(z, p, e), flat((z + LATE) % FS, e // 2, (2 * e + p) % EP))
+        for z in range(FS)
+        for p in range(PP)
+        for e in range(EP)
+    ]
+
+
 def solution(mesh):
     in_spec = P("pp", "ep", None, "fs")
     down_spec = P("pp", "ep", "fs", None)
@@ -321,7 +412,12 @@
         exp_local = w_gate.shape[1]
         offset = jnp.clip(hot_ids - lax.axis_index("ep") * exp_local, 0, exp_local - 1)
         picked = pick(w_gate, w_up, w_down, offset)
-        return exchange(hot_ids, w_gate, w_up, w_down, *picked)
+        *came, late = exchange(hot_ids, w_gate, w_up, w_down, *picked)
+        late = lax.ppermute(late, ("fs", "pp", "ep"), late_pairs())
+        w13, w2, hot13, hot2 = settle(*came)
+        core, z = lax.rem(lax.axis_index("ep"), 2), lax.axis_index("fs")
+        w2 = insert(w2, late, core, lax.rem(z + LATE, FS))
+        return w13, w2, hot13, hot2
 
     return jax.shard_map(
         device_body,

time: 628 us -> 491 us (0.78)
  Pallas kernels: 583 us -> 488 us
  local copies, waits for them, and re-layouts: 41.3 us -> 0.89 us
    pallas_call x1, Pallas kernels: 577 us -> 441 us  [exchange(): pl.pallas_call(functools.partial(exchange_body, exp_local), out_shape=(ja...]
    pallas_call x0 -> x2, Pallas kernels: none -> 40.8 us  [the longest x1 37.3 us: settle(): pl.pallas_call(functools.partial(settle_body, n_slot, ahead), out_shape=t...]
    unnamed x12 -> x2, local copies, waits for them, and re-layouts: 41.3 us -> 0.89 us
  transfers between devices with their start and end apart: 0 -> 1, of which waited for: 0 -> 0; matrix products, arithmetic and copies ran while one was open for 0% -> 0% of each run, Pallas kernels for 0% -> 8%
where the time goes in v2:
time: 491 us
  Pallas kernels  488 us (99%)
    pallas_call x1, Pallas kernels, exchange(): pl.pallas_call(functools.partial(exchange_body, exp_local), out_shape=(ja...  441 us
    pallas_call x1, Pallas kernels, settle(): pl.pallas_call(functools.partial(settle_body, n_slot, ahead), out_shape=t...  37.3 us
  transfers between devices with their start and end apart: 1, of which 0 were waited for; matrix products, arithmetic and copies ran while one was open for 0% of the time, Pallas kernels for 8%

profile of v2, /device:TPU:0, one launch (start us, length us, event | category | flops | bytes accessed | tf_op | source)
XLA Modules:
  0.0 491.0 jit_solution(8283584374849508289)
XLA Ops:
  0.6 1.2 subtract_clamp_fusion.off_ref
  1.8 5.7 %pick.1 = (bf16[6,1024,128]{2,1,0:T(8,128)(2,1)}, bf16[6,1024,128]{2,1,0:T(8,128)(2,1)}, bf16[6,128,1024]{2,1,0:T(8,128)(2,1)}) custom-call(s32[6]{0:T(128)} %subtract_clamp_fusion.off_ref, bf16[1,24,1024,128]{3,2,1,0:T(8,128)(2,1)} %gate.1, bf16[1,24,1024,128]{3,2,1,0:T(8,128)(2,1)} %up.1, bf16[1,24,128,1024]{3,2,1,0:T(8,128)(2,1)} %down.1), custom_call_target="tpu_custom_call" | custom-call | tf_op jit(solution)/shard_map/pick/pallas_call | solution.py:30
  7.5 441.1 %exchange.1 = (bf16[2,3,1024,1024]{3,2,1,0:T(8,128)(2,1)}, bf16[2,3,512,1024]{3,2,1,0:T(8,128)(2,1)}, bf16[2,6,1024,1024]{3,2,1,0:T(8,128)(2,1)}, bf16[2,6,512,1024]{3,2,1,0:T(8,128)(2,1)}, bf16[3,128,1024]{2,1,0:T(8,128)(2,1)}) custom-call(s32[6]{0:T(128)} %ids.1, bf16[1,24,1024,128]{3,2,1,0:T(8,128)(2,1)} %gate.1, bf16[1,24,1024,128]{3,2,1,0:T(8,128)(2,1)} %up.1, ...), custom_call_target="tpu_custom_call" | custom-call | tf_op jit(solution)/shard_map/exchange/pallas_call | solution.py:310
  448.6 0.1 collective-permute-start
  448.7 37.3 %settle.1 = (bf16[2,3,1024,1024]{3,2,1,0:T(8,128)(2,1)}, bf16[2,3,512,1024]{3,2,1,0:T(8,128)(2,1)}, bf16[2,6,1024,1024]{3,2,1,0:T(8,128)(2,1)}, bf16[2,6,512,1024]{3,2,1,0:T(8,128)(2,1)}) custom-call(bf16[2,3,1024,1024]{3,2,1,0:T(8,128)(2,1)} %get-tuple-element.19.refs_0_, bf16[2,3,512,1024]{3,2,1,0:T(8,128)(2,1)} %get-tuple-element.20.refs_1_, ...), custom_call_target="tpu_custom_call" | custom-call | flops 905969664 | bytes 113246208 | tf_op jit(solution)/shard_map/settle/pallas_call | solution.py:361
  486.0 0.6 pad_add_fusion.at_ref
  486.6 0.0 collective-permute-done.piece_in
  486.6 0.0 copy-start
  486.6 0.9 copy-done
  487.5 3.5 insert.1
Async XLA Ops:
  448.6 38.0 %collective-permute-start = (bf16[3,128,1024]{2,1,0:T(8,128)(2,1)}, bf16[3,128,1024]{2,1,0:T(8,128)(2,1)S(1)}, u32[]{:S(2)}, u32[]{:S(2)}) collective-permute-start(bf16[3,128,1024]{2,1,0:T(8,128)(2,1)} %get-tuple-element.24), channel_id=1, source_target_pairs={{0,16},{1,18},{2,20},{3,22},{4,17},{5,19},{6,21},{7,23},{8,24},{9,... | collective-permute-start | bytes 2359304 | tf_op jit(solution)/shard_map/ppermute | solution.py:416
  486.6 0.9 copy-start

commit v3 on v2

--- a/solution.py
+++ b/solution.py
@@ -8,45 +8,56 @@
 from jax.sharding import PartitionSpec as P
 
 ANY = pl.BlockSpec(memory_space=pl.ANY)
+HBM = pl.BlockSpec(memory_space=pltpu.HBM)
+VMEM = pl.BlockSpec(memory_space=pltpu.VMEM)
 MESH = pl.DeviceIdType.MESH
 FS, PP, EP = 4, 2, 4
 N_T = 3
 LATE = 2
-ORDER = [(kk, b, t) for t in range(N_T) for b in range(2) for kk in (1, 3, 2, 0) if (kk, b, t) != (LATE, 1, 2)]
-BATCH = (8, 0, 0, 0, 0)
-
-
-def pick_body(off_ref, gate_in, up_in, down_in, gate_out, up_out, down_out):
-    gate_out[...] = gate_in[0]
-    up_out[...] = up_in[0]
-    down_out[...] = down_in[0]
-
-
-def pick(w_gate, w_up, w_down, offset):
-    hot = offset.shape[0]
-    d, f = w_gate.shape[2:]
-    src = lambda a, b: pl.BlockSpec((1, 1, a, b), lambda h, off: (0, off[h], 0, 0))
-    dst = lambda a, b: pl.BlockSpec((1, a, b), lambda h, off: (h, 0, 0))
+OUTER = [(m, b, t) for t in range(N_T) for b in range(2) for m in (1, 3, 2, 0) if (m, b, t) != (2, 1, 2)]
+INNER = [(m, b, t) for t in range(N_T) for b in range(2) for m in (2, 0, 3, 1) if (m, b, t) != (3, 1, 2)]
+COUNTS = (6, 0, 0, 0, 24)
+
+
+def in_hbm(a):
+    return pltpu.with_memory_space_constraint(a, pltpu.HBM)
+
+
+def in_vmem(a):
+    return pltpu.with_memory_space_constraint(a, pltpu.VMEM)
+
+
+def pick_body(exp_per_ep, ids, gate, up, down, gate_out, up_out, down_out, sems):
+    base = lax.axis_index("ep") * exp_per_ep
+    copies = []
+    for h in range(gate_out.shape[0]):
+        held = jnp.clip(ids[h] - base, 0, exp_per_ep - 1)
+        for t, (s, d) in enumerate(((gate, gate_out), (up, up_out), (down, down_out))):
+            copies.append(pltpu.make_async_copy(s.at[0, held], d.at[h], sems.at[h * N_T + t]))
+    for copy in copies:
+        copy.start()
+    for copy in copies:
+        copy.wait()
+
+
+def pick(ids, w_gate, w_up, w_down):
+    hot = ids.shape[0]
+    exp_local, d, f = w_gate.shape[1:]
+    dt = w_gate.dtype
     return pl.pallas_call(
-        pick_body,
-        out_shape=(
-            jax.ShapeDtypeStruct((hot, d, f), w_gate.dtype),
-            jax.ShapeDtypeStruct((hot, d, f), w_gate.dtype),
-            jax.ShapeDtypeStruct((hot, f, d), w_gate.dtype),
-        ),
-        grid_spec=pltpu.PrefetchScalarGridSpec(
-            num_scalar_prefetch=1,
-            grid=(hot,),
-            in_specs=[src(d, f), src(d, f), src(f, d)],
-            out_specs=[dst(d, f), dst(d, f), dst(f, d)],
-        ),
+        functools.partial(pick_body, exp_local),
+        out_shape=(pltpu.VMEM((hot, d, f), dt), pltpu.VMEM((hot, d, f), dt), pltpu.VMEM((hot, f, d), dt)),
+        in_specs=[pl.BlockSpec(memory_space=pltpu.SMEM)] + [HBM] * N_T,
+        out_specs=(pl.BlockSpec(memory_space=pltpu.VMEM),) * N_T,
+        scratch_shapes=[pltpu.SemaphoreType.DMA((hot * N_T,))],
+        compiler_params=pltpu.CompilerParams(vmem_limit_bytes=4 << 20),
         name="pick",
-    )(offset, w_gate, w_up, w_down)
+    )(ids, w_gate, w_up, w_down)
 
 
 def exchange_body(
     exp_per_ep, ids, gate, up, down, hot_g, hot_u, hot_d, w13, w2, hot13, hot2, late,
-    cand_g, cand_u, cand_d, sel_g, sel_u, sel_d,
+    got_g, got_u, got_d, got_xg, got_xu, got_xd, snd_g, snd_u, snd_d, keep_g, keep_u, keep_d, sel_g, sel_u, sel_d,
     main_s, main_r, rs_s, rs_r, loc, own, z_s, z_r, x_s, x_r, y_s, y_r, p_s, p_r, da_s, da_r, db_s, db_r, px_s, px_r, py_s, py_r, pa_s, pa_r, pb_s, pb_r,
 ):
     z, p, e = lax.axis_index("fs"), lax.axis_index("pp"), lax.axis_index("ep")
@@ -104,16 +115,27 @@
         def _():
             pltpu.make_async_copy(s, d, loc.at[t]).wait()
 
-    queue = [(lax.rem(z + kk, FS), 1 - p if (kk, t) == (LATE, 2) else b, t) for kk, b, t in ORDER]
+    upper = z // 2
+    inner = z * (1 - upper) + (FS - 1 - z) * upper
+
+    def group(items, late_plane):
+        for m, b, t in items:
+            b = 1 - p if t == 2 and m == late_plane else b
+            main_start(m * (1 - upper) + (FS - 1 - m) * upper, b, t)
+
+    bounds = [0]
+
+    def after_step():
+        lo = bounds[-1]
+        step = len(bounds) - 1
+        hi = min(len(OUTER), lo + (COUNTS[step] if step < len(COUNTS) else len(OUTER)))
+        bounds.append(hi)
+        if hi > lo:
+            pl.when(inner == 0)(lambda: group(OUTER[lo:hi], LATE))
+            pl.when(inner == 1)(lambda: group(INNER[lo:hi], LATE + 1))
+
     late_src = down.at[0, pl.ds(3 * (p * FS + lax.rem(z + LATE, FS)), 3)]
     pltpu.make_async_copy(late_src, late, loc.at[N_T]).start()
-    started = []
-
-    def main_next(n):
-        for item in queue[len(started) : len(started) + n]:
-            main_start(*item)
-            started.append(item)
-
     def main_landed(ys, zs):
         mine = jnp.logical_and(jnp.logical_and(2 * p + x == e, p == ys), z == zs)
 
@@ -158,30 +180,39 @@
             hot_d.at[:, pl.ds(pl.multiple_of(q * cut_d, cut_d), cut_d), :],
         )
 
-    def cand(q):
-        return cand_g.at[q], cand_u.at[q], cand_d.at[q]
-
-    for k in range(1, EP):
-        q = lax.rem(e + k, EP)
-        for t in range(N_T):
-            remote(part(q)[t], cand(e)[t], rs_s.at[k * N_T + t], rs_r.at[k * N_T + t], (z, p, q)).start()
+    got = (got_g, got_u, got_d)
+    got_x = (got_xg, got_xu, got_xd)
+    snd = (snd_g, snd_u, snd_d)
+    keep = (keep_g, keep_u, keep_d)
+    picked = (hot_g, hot_u, hot_d)
+    cut = (cut_g, cut_g, cut_d)
+    for xx in range(2):
+        for t in range(N_T):
+            i = xx * N_T + t
+            remote(part(2 * xx + 1 - c)[t], got[t].at[xx], rs_s.at[i], rs_r.at[i], to_p).start()
+    after_step()
+    for xx in range(2):
+        for t in range(N_T):
+            landed(got[t].at[xx], rs_r.at[xx * N_T + t])
+
+    def of_chip(xx, out):
+        for h in range(hot):
+            here = lax.rem(ids[h] // exp_per_ep, 2) == c
+            for t in range(N_T):
+                rows = pl.ds(pl.multiple_of((2 * xx + c) * cut[t], cut[t]), cut[t])
+                out[t][h] = jnp.where(here, picked[t][h, rows, :], got[t][xx, h])
+
+    of_chip(1 - x, snd)
+    of_chip(x, keep)
     for t in range(N_T):
-        pltpu.make_async_copy(part(e)[t], cand(e)[t], own.at[t]).start()
-
-    main_next(BATCH[0])
-
+        i = 2 * N_T + t
+        remote(snd[t], got_x[t], rs_s.at[i], rs_r.at[i], to_x).start()
     for t in range(N_T):
-        pltpu.make_async_copy(part(e)[t], cand(e)[t], own.at[t]).wait()
-    for k in range(1, EP):
-        q = lax.rem(e + EP - k, EP)
-        for t in range(N_T):
-            landed(cand(q)[t], rs_r.at[k * N_T + t])
-
+        landed(got_x[t], rs_r.at[2 * N_T + t])
     for h in range(hot):
-        holder = ids[h] // exp_per_ep
-        sel_g[h] = cand_g[holder, h]
-        sel_u[h] = cand_u[holder, h]
-        sel_d[h] = cand_d[holder, h]
+        here = ids[h] // exp_per_ep // 2 == x
+        for t in range(N_T):
+            (sel_g, sel_u, sel_d)[t][h] = jnp.where(here, keep[t][h], got_x[t][h])
     sel = (sel_g, sel_u, sel_d)
 
     def broadcast(src, zz, k):
@@ -201,8 +232,8 @@
     def _():
         send(sel, mine, z_s, z_r, DOWN * FS + 1, (z - 1, p, e))
 
-    main_next(BATCH[1])
     broadcast(sel, z, z)
+    after_step()
     for t in range(N_T):
         pltpu.make_async_copy(sel[t], mine[t], own.at[t]).start()
 
@@ -251,19 +282,20 @@
 
     for k in range(1, FS):
         z_step(k)
-        main_next(BATCH[1 + k])
-    main_next(len(queue))
+        after_step()
     for k in range(FS):
         plane_step(lax.rem(z + k, FS))
+        after_step()
     for k in range(FS):
         diagonal_step(lax.rem(z + k, FS))
+        after_step()
+    after_step()
 
     for t in range(N_T):
         pltpu.make_async_copy(sel[t], mine[t], own.at[t]).wait()
-    for k in range(1, EP):
-        q = lax.rem(e + k, EP)
-        for t in range(N_T):
-            remote(part(q)[t], cand(e)[t], rs_s.at[k * N_T + t], rs_s.at[k * N_T + t], (z, p, q)).wait_send()
+    for i in range(3 * N_T):
+        t = i % N_T
+        remote(sel[t], sel[t], rs_s.at[i], rs_s.at[i], to_p).wait_send()
     for k in range(1, FS):
         @pl.when(jnp.logical_and(z - k + 1 >= 0, z < FS - 1))
         def _():
@@ -280,18 +312,25 @@
         sent(src, px_s, zz, to_p)
         sent(src, py_s, zz, to_p)
         a = piece(p, q_x, zz, 0, half)
+        b = piece(p, q_x, zz, half, hot)
         sent(a, da_s, zz, to_y)
-        sent(a, db_s, zz, to_x)
+        sent(b, db_s, zz, to_x)
         sent(a, pa_s, zz, to_p)
-        sent(a, pb_s, zz, to_p)
+        sent(b, pb_s, zz, to_p)
         q_px = 2 * (1 - x) + (1 - c)
         arrived(piece(p, q_p, zz), p_r, zz)
         arrived(piece(p, q_px, zz), px_r, zz)
         arrived(piece(1 - p, q_p, zz), py_r, zz)
         arrived(piece(1 - p, q_px, zz, 0, half), pa_r, zz)
         arrived(piece(1 - p, q_px, zz, half, hot), pb_r, zz)
-    for item in queue:
-        main_sent(*item)
+    for t in range(N_T):
+        for kk in range(FS):
+            zz = lax.rem(z + kk, FS)
+            if (kk, t) == (LATE, 2):
+                main_sent(zz, 1 - p, t)
+            else:
+                main_sent(zz, 0, t)
+                main_sent(zz, 1, t)
     pltpu.make_async_copy(late_src, late, loc.at[N_T]).wait()
     for ys in range(PP):
         for zs in range(FS):
@@ -310,20 +349,20 @@
     return pl.pallas_call(
         functools.partial(exchange_body, exp_local),
         out_shape=(
-            jax.ShapeDtypeStruct((PP, per_dev, d, 2 * full), dt),
-            jax.ShapeDtypeStruct((PP, per_dev, full, d), dt),
-            jax.ShapeDtypeStruct((PP, hot, d, 2 * full), dt),
-            jax.ShapeDtypeStruct((PP, hot, full, d), dt),
-            jax.ShapeDtypeStruct((per_dev, f, d), dt),
+            pltpu.HBM((PP, per_dev, d, 2 * full), dt),
+            pltpu.HBM((PP, per_dev, full, d), dt),
+            pltpu.HBM((PP, hot, d, 2 * full), dt),
+            pltpu.HBM((PP, hot, full, d), dt),
+            pltpu.HBM((per_dev, f, d), dt),
         ),
-        in_specs=[pl.BlockSpec(memory_space=pltpu.SMEM)] + [ANY] * 6,
-        out_specs=(ANY,) * 5,
-        scratch_shapes=[pltpu.VMEM((EP,) + s, dt) for s in quarter]
-        + [pltpu.VMEM(s, dt) for s in quarter]
+        in_specs=[pl.BlockSpec(memory_space=pltpu.SMEM)] + [HBM] * N_T + [VMEM] * N_T,
+        out_specs=(HBM,) * 5,
+        scratch_shapes=[pltpu.VMEM((2,) + s, dt) for s in quarter]
+        + [pltpu.VMEM(s, dt) for s in quarter] * 4
         + [dma(FS * PP * N_T), dma(FS * PP * N_T), dma(EP * N_T), dma(EP * N_T), dma(N_T + 1), dma(N_T)]
         + [dma(2 * FS * N_T), dma(2 * FS * N_T)]
         + four() * 9,
-        compiler_params=pltpu.CompilerParams(has_side_effects=True),
+        compiler_params=pltpu.CompilerParams(has_side_effects=True, vmem_limit_bytes=16 << 20),
         name="exchange",
     )(ids, w_gate, w_up, w_down, hot_g, hot_u, hot_d)
 
@@ -361,8 +400,8 @@
     return pl.pallas_call(
         functools.partial(settle_body, n_slot, ahead),
         out_shape=tuple(jax.ShapeDtypeStruct(a.shape, a.dtype) for a in arrays),
-        in_specs=[ANY] * len(arrays),
-        out_specs=(ANY,) * len(arrays),
+        in_specs=[HBM] * len(arrays),
+        out_specs=(HBM,) * len(arrays),
         scratch_shapes=[
             pltpu.VMEM((n_slot, rows, arrays[0].shape[3]), arrays[0].dtype),
             pltpu.SemaphoreType.DMA((n_slot,)),
@@ -373,24 +412,26 @@
     )(*arrays)
 
 
-def insert_body(at_ref, piece_in, whole_in, whole_out):
-    whole_out[0] = piece_in[...]
-
-
-def insert(whole, piece, lay, zz):
-    _, f, d = piece.shape
+def insert_body(piece, whole_in, whole_out, sem):
+    f = piece.shape[1]
+    lay, zz = lax.rem(lax.axis_index("ep"), 2), lax.rem(lax.axis_index("fs") + LATE, FS)
+    at = whole_out.at[lay, :, pl.ds(pl.multiple_of(zz * f, f), f), :]
+    copy = pltpu.make_async_copy(piece, at, sem)
+    copy.start()
+    copy.wait()
+
+
+def insert(whole, piece):
     return pl.pallas_call(
         insert_body,
         out_shape=jax.ShapeDtypeStruct(whole.shape, whole.dtype),
-        grid_spec=pltpu.PrefetchScalarGridSpec(
-            num_scalar_prefetch=1,
-            grid=(piece.shape[0],),
-            in_specs=[pl.BlockSpec((1, f, d), lambda h, at: (h, 0, 0)), ANY],
-            out_specs=pl.BlockSpec((1, 1, f, d), lambda h, at: (at[0], h, at[1], 0)),
-        ),
-        input_output_aliases={2: 0},
+        in_specs=[pl.BlockSpec(memory_space=pltpu.VMEM), HBM],
+        out_specs=HBM,
+        scratch_shapes=[pltpu.SemaphoreType.DMA],
+        compiler_params=pltpu.CompilerParams(vmem_limit_bytes=4 << 20),
+        input_output_aliases={1: 0},
         name="insert",
-    )(jnp.stack([lay, zz]), piece, whole)
+    )(piece, whole)
 
 
 def late_pairs():
@@ -409,14 +450,12 @@
     home_spec = P(None, ("pp", "ep", "fs"), None, None)
 
     def device_body(w_gate, w_up, w_down, hot_ids):
-        exp_local = w_gate.shape[1]
-        offset = jnp.clip(hot_ids - lax.axis_index("ep") * exp_local, 0, exp_local - 1)
-        picked = pick(w_gate, w_up, w_down, offset)
+        w_gate, w_up, w_down = in_hbm(w_gate), in_hbm(w_up), in_hbm(w_down)
+        picked = map(in_vmem, pick(hot_ids, w_gate, w_up, w_down))
         *came, late = exchange(hot_ids, w_gate, w_up, w_down, *picked)
         late = lax.ppermute(late, ("fs", "pp", "ep"), late_pairs())
         w13, w2, hot13, hot2 = settle(*came)
-        core, z = lax.rem(lax.axis_index("ep"), 2), lax.axis_index("fs")
-        w2 = insert(w2, late, core, lax.rem(z + LATE, FS))
+        w2 = insert(w2, late)
         return w13, w2, hot13, hot2
 
     return jax.shard_map(

time: 491 us -> 480 us (0.978)
  Pallas kernels: 488 us -> 471 us
  starting transfers between devices: 0.06 us -> 6.73 us
    pallas_call x2, Pallas kernels: 447 us -> 433 us  [the longest x1 430 us: exchange(): pl.pallas_call(functools.partial(exchange_body, exp_local), out_shape=(pl...]
    ppermute x1, starting transfers between devices: 0.06 us -> 6.73 us  [device_body(): late = lax.ppermute(late, ('fs', 'pp', 'ep'), late_pairs())]
where the time goes in v3:
time: 480 us; the launch traced here: 479 us
  Pallas kernels  471 us (98%)
  starting transfers between devices  6.73 us (1%)
    pallas_call x1, Pallas kernels, exchange(): pl.pallas_call(functools.partial(exchange_body, exp_local), out_shape=(pl...  430 us
    pallas_call x1, Pallas kernels, settle(): pl.pallas_call(functools.partial(settle_body, n_slot, ahead), out_shape=t...  37.2 us
  transfers between devices with their start and end apart: 1, of which 0 were waited for; matrix products, arithmetic and copies ran while one was open for 0% of the time, Pallas kernels for 8%

profile of v3, /device:TPU:0, one launch (start us, length us, event | category | flops | bytes accessed | tf_op | source)
XLA Modules:
  0.0 479.0 jit_solution(16544950322010873832)
XLA Ops:
  0.6 0.0 copy-start
  0.6 0.6 copy-done
  1.3 0.0 copy-start.1
  1.3 3.0 pick.1
  4.3 0.0 copy-done.1
  4.3 429.8 %exchange.1 = (bf16[2,3,1024,1024]{3,2,1,0:T(8,128)(2,1)}, bf16[2,3,512,1024]{3,2,1,0:T(8,128)(2,1)}, bf16[2,6,1024,1024]{3,2,1,0:T(8,128)(2,1)}, bf16[2,6,512,1024]{3,2,1,0:T(8,128)(2,1)}, bf16[3,128,1024]{2,1,0:T(8,128)(2,1)}) custom-call(s32[6]{0:T(128)S(1)} %copy-done.1, bf16[1,24,1024,128]{3,2,1,0:T(8,128)(2,1)} %gate.3, bf16[1,24,1024,128]{3,2,1,0:T(8,128)(2,1)} %up.3, ...), custom_call_target="tpu_custom_call" | custom-call | tf_op jit(solution)/shard_map/exchange/pallas_call | solution.py:349
  434.1 6.7 %collective-permute-start = (bf16[3,128,1024]{2,1,0:T(8,128)(2,1)}, bf16[3,128,1024]{2,1,0:T(8,128)(2,1)S(1)}, u32[]{:S(2)}, u32[]{:S(2)}) collective-permute-start(bf16[3,128,1024]{2,1,0:T(8,128)(2,1)} %get-tuple-element.24), channel_id=1, source_target_pairs={{0,16},{1,18},{2,20},{3,22},{4,17},{5,19},{6,21},{7,23},{8,24},{9,... | collective-permute-start | bytes 2359304 | tf_op jit(solution)/shard_map/ppermute | solution.py:456
  440.9 37.2 %settle.1 = (bf16[2,3,1024,1024]{3,2,1,0:T(8,128)(2,1)}, bf16[2,3,512,1024]{3,2,1,0:T(8,128)(2,1)}, bf16[2,6,1024,1024]{3,2,1,0:T(8,128)(2,1)}, bf16[2,6,512,1024]{3,2,1,0:T(8,128)(2,1)}) custom-call(bf16[2,3,1024,1024]{3,2,1,0:T(8,128)(2,1)} %get-tuple-element.19.refs_0_, bf16[2,3,512,1024]{3,2,1,0:T(8,128)(2,1)} %get-tuple-element.20.refs_1_, ...), custom_call_target="tpu_custom_call" | custom-call | flops 905969664 | bytes 113246208 | tf_op jit(solution)/shard_map/settle/pallas_call | solution.py:400
  478.1 0.0 collective-permute-done.piece
  478.1 0.9 insert.1
Async XLA Ops:
  0.6 0.7 copy-start
  1.3 3.1 copy-start.1
  434.1 44.0 %collective-permute-start = (bf16[3,128,1024]{2,1,0:T(8,128)(2,1)}, bf16[3,128,1024]{2,1,0:T(8,128)(2,1)S(1)}, u32[]{:S(2)}, u32[]{:S(2)}) collective-permute-start(bf16[3,128,1024]{2,1,0:T(8,128)(2,1)} %get-tuple-element.24), channel_id=1, source_target_pairs={{0,16},{1,18},{2,20},{3,22},{4,17},{5,19},{6,21},{7,23},{8,24},{9,... | collective-permute-start | bytes 2359304 | tf_op jit(solution)/shard_map/ppermute | solution.py:456

commit v4 on v3

--- a/solution.py
+++ b/solution.py
@@ -14,9 +14,9 @@
 FS, PP, EP = 4, 2, 4
 N_T = 3
 LATE = 2
-OUTER = [(m, b, t) for t in range(N_T) for b in range(2) for m in (1, 3, 2, 0) if (m, b, t) != (2, 1, 2)]
-INNER = [(m, b, t) for t in range(N_T) for b in range(2) for m in (2, 0, 3, 1) if (m, b, t) != (3, 1, 2)]
-COUNTS = (6, 0, 0, 0, 24)
+OUTER = [(m, b, t) for t in range(N_T) for b in range(2) for m in (1, 3, 2, 0) if (m, t) != (2, 2)]
+INNER = [(m, b, t) for t in range(N_T) for b in range(2) for m in (2, 0, 3, 1) if (m, t) != (3, 2)]
+COUNTS = (4, 0, 0, 0, 24)
 
 
 def in_hbm(a):
@@ -118,9 +118,8 @@
     upper = z // 2
     inner = z * (1 - upper) + (FS - 1 - z) * upper
 
-    def group(items, late_plane):
+    def group(items):
         for m, b, t in items:
-            b = 1 - p if t == 2 and m == late_plane else b
             main_start(m * (1 - upper) + (FS - 1 - m) * upper, b, t)
 
     bounds = [0]
@@ -131,17 +130,17 @@
         hi = min(len(OUTER), lo + (COUNTS[step] if step < len(COUNTS) else len(OUTER)))
         bounds.append(hi)
         if hi > lo:
-            pl.when(inner == 0)(lambda: group(OUTER[lo:hi], LATE))
-            pl.when(inner == 1)(lambda: group(INNER[lo:hi], LATE + 1))
+            pl.when(inner == 0)(lambda: group(OUTER[lo:hi]))
+            pl.when(inner == 1)(lambda: group(INNER[lo:hi]))
 
     late_src = down.at[0, pl.ds(3 * (p * FS + lax.rem(z + LATE, FS)), 3)]
     pltpu.make_async_copy(late_src, late, loc.at[N_T]).start()
     def main_landed(ys, zs):
         mine = jnp.logical_and(jnp.logical_and(2 * p + x == e, p == ys), z == zs)
 
-        is_late = jnp.logical_and(ys == c, zs == lax.rem(z + LATE, FS))
+        outside = zs == lax.rem(z + LATE, FS)
         for t, d in enumerate(home(ys, zs)):
-            skip = jnp.logical_or(mine, is_late) if t == 2 else mine
+            skip = jnp.logical_or(mine, outside) if t == 2 else mine
 
             @pl.when(jnp.logical_not(skip))
             def _():
@@ -326,9 +325,7 @@
     for t in range(N_T):
         for kk in range(FS):
             zz = lax.rem(z + kk, FS)
-            if (kk, t) == (LATE, 2):
-                main_sent(zz, 1 - p, t)
-            else:
+            if (kk, t) != (LATE, 2):
                 main_sent(zz, 0, t)
                 main_sent(zz, 1, t)
     pltpu.make_async_copy(late_src, late, loc.at[N_T]).wait()
@@ -352,71 +349,93 @@
             pltpu.HBM((PP, per_dev, d, 2 * full), dt),
             pltpu.HBM((PP, per_dev, full, d), dt),
             pltpu.HBM((PP, hot, d, 2 * full), dt),
-            pltpu.HBM((PP, hot, full, d), dt),
+            pltpu.VMEM((PP, hot, full, d), dt),
             pltpu.HBM((per_dev, f, d), dt),
         ),
         in_specs=[pl.BlockSpec(memory_space=pltpu.SMEM)] + [HBM] * N_T + [VMEM] * N_T,
-        out_specs=(HBM,) * 5,
+        out_specs=(HBM, HBM, HBM, VMEM, HBM),
         scratch_shapes=[pltpu.VMEM((2,) + s, dt) for s in quarter]
         + [pltpu.VMEM(s, dt) for s in quarter] * 4
         + [dma(FS * PP * N_T), dma(FS * PP * N_T), dma(EP * N_T), dma(EP * N_T), dma(N_T + 1), dma(N_T)]
         + [dma(2 * FS * N_T), dma(2 * FS * N_T)]
         + four() * 9,
         compiler_params=pltpu.CompilerParams(has_side_effects=True, vmem_limit_bytes=16 << 20),
+        cost_estimate=pl.CostEstimate(flops=1 << 36, bytes_accessed=1 << 27, transcendentals=0),
         name="exchange",
     )(ids, w_gate, w_up, w_down, hot_g, hot_u, hot_d)
 
 
-def settle_body(n_slot, ahead, *refs):
-    n = (len(refs) - 3) // 2
-    src, dst, (buf, r_sem, w_sem) = refs[:n], refs[n : 2 * n], refs[2 * n :]
-    steps = [(a, i, j) for a in range(n) for i in range(src[a].shape[0]) for j in range(src[a].shape[1])]
+def place_of(piece, whole, lay):
+    f = piece.shape[1]
+    zz = lax.rem(lax.axis_index("fs") + LATE, FS)
+    return whole.at[lay, :, pl.ds(pl.multiple_of(zz * f, f), f), :]
+
+
+def settle_body(n_slot, ahead, w13, w2, hot13, hot2, early, w13_out, w2_out, hot13_out, hot2_out, buf, r_sem, w_sem, hot_sem, early_sem):
+    steps = [
+        (src, dst, i, j)
+        for src, dst in ((w2, w2_out), (w13, w13_out), (hot13, hot13_out))
+        for i in range(src.shape[0])
+        for j in range(src.shape[1])
+    ]
+    n_first = w2.shape[0] * w2.shape[1]
+    direct = [pltpu.make_async_copy(hot2.at[i], hot2_out.at[i], hot_sem.at[i]) for i in range(hot2.shape[0])]
+    core = lax.rem(lax.axis_index("ep"), 2)
+    early_copy = pltpu.make_async_copy(early, place_of(early, w2_out, 1 - core), early_sem)
 
     def load(k):
-        a, i, j = steps[k]
-        return pltpu.make_async_copy(src[a].at[i, j], buf.at[k % n_slot, pl.ds(0, src[a].shape[2])], r_sem.at[k % n_slot])
+        src, dst, i, j = steps[k]
+        return pltpu.make_async_copy(src.at[i, j], buf.at[k % n_slot, pl.ds(0, src.shape[2])], r_sem.at[k % n_slot])
 
     def store(k):
-        a, i, j = steps[k]
-        return pltpu.make_async_copy(buf.at[k % n_slot, pl.ds(0, src[a].shape[2])], dst[a].at[i, j], w_sem.at[k % n_slot])
-
-    for k in range(min(ahead, len(steps))):
+        src, dst, i, j = steps[k]
+        return pltpu.make_async_copy(buf.at[k % n_slot, pl.ds(0, src.shape[2])], dst.at[i, j], w_sem.at[k % n_slot])
+
+    for k in range(ahead):
         load(k).start()
+    for copy in direct:
+        copy.start()
     for k in range(len(steps)):
         load(k).wait()
         store(k).start()
         if k + ahead < len(steps):
-            if k + ahead >= n_slot:
-                store(k + ahead - n_slot).wait()
+            old = k + ahead - n_slot
+            if old >= 0:
+                store(old).wait()
+            if old == n_first - 1:
+                early_copy.start()
             load(k + ahead).start()
-    for k in range(max(0, len(steps) - n_slot), len(steps)):
+    for k in range(len(steps) - n_slot, len(steps)):
         store(k).wait()
-
-
-def settle(*arrays):
-    n_slot, ahead = 12, 6
-    rows = max(a.shape[2] for a in arrays)
+    for copy in direct:
+        copy.wait()
+    early_copy.wait()
+
+
+def settle(w13, w2, hot13, hot2, early):
+    n_slot, ahead = 12, 7
+    arrays = [in_hbm(w13), in_hbm(w2), in_hbm(hot13), in_vmem(hot2)]
     size = sum(a.size * a.dtype.itemsize for a in arrays)
     return pl.pallas_call(
         functools.partial(settle_body, n_slot, ahead),
-        out_shape=tuple(jax.ShapeDtypeStruct(a.shape, a.dtype) for a in arrays),
-        in_specs=[HBM] * len(arrays),
+        out_shape=tuple(pltpu.HBM(a.shape, a.dtype) for a in arrays),
+        in_specs=[HBM, HBM, HBM, VMEM, VMEM],
         out_specs=(HBM,) * len(arrays),
         scratch_shapes=[
-            pltpu.VMEM((n_slot, rows, arrays[0].shape[3]), arrays[0].dtype),
+            pltpu.VMEM((n_slot,) + w13.shape[2:], w13.dtype),
             pltpu.SemaphoreType.DMA((n_slot,)),
             pltpu.SemaphoreType.DMA((n_slot,)),
+            pltpu.SemaphoreType.DMA((PP,)),
+            pltpu.SemaphoreType.DMA,
         ],
+        compiler_params=pltpu.CompilerParams(vmem_limit_bytes=26 << 20),
         cost_estimate=pl.CostEstimate(flops=size * 16, bytes_accessed=2 * size, transcendentals=0),
         name="settle",
-    )(*arrays)
+    )(*arrays, early)
 
 
 def insert_body(piece, whole_in, whole_out, sem):
-    f = piece.shape[1]
-    lay, zz = lax.rem(lax.axis_index("ep"), 2), lax.rem(lax.axis_index("fs") + LATE, FS)
-    at = whole_out.at[lay, :, pl.ds(pl.multiple_of(zz * f, f), f), :]
-    copy = pltpu.make_async_copy(piece, at, sem)
+    copy = pltpu.make_async_copy(piece, place_of(piece, whole_out, lax.rem(lax.axis_index("ep"), 2)), sem)
     copy.start()
     copy.wait()
 
@@ -434,10 +453,31 @@
     )(piece, whole)
 
 
-def late_pairs():
+def stage_body(down, out, sem):
+    z, p = lax.axis_index("fs"), lax.axis_index("pp")
+    n = out.shape[0]
+    copy = pltpu.make_async_copy(down.at[0, pl.ds(n * ((1 - p) * FS + lax.rem(z + LATE, FS)), n)], out, sem)
+    copy.start()
+    copy.wait()
+
+
+def stage(w_down):
+    exp_local, f, d = w_down.shape[1:]
+    return pl.pallas_call(
+        stage_body,
+        out_shape=pltpu.VMEM((exp_local // (FS * PP), f, d), w_down.dtype),
+        in_specs=[HBM],
+        out_specs=VMEM,
+        scratch_shapes=[pltpu.SemaphoreType.DMA],
+        compiler_params=pltpu.CompilerParams(vmem_limit_bytes=4 << 20),
+        name="stage",
+    )(w_down)
+
+
+def piece_pairs(core_of_stage):
     flat = lambda z, p, e: (z * PP + p) * EP + e
     return [
-        (flat(z, p, e), flat((z + LATE) % FS, e // 2, (2 * e + p) % EP))
+        (flat(z, p, e), flat((z + LATE) % FS, e // 2, (2 * e + core_of_stage(p)) % EP))
         for z in range(FS)
         for p in range(PP)
         for e in range(EP)
@@ -451,10 +491,11 @@
 
     def device_body(w_gate, w_up, w_down, hot_ids):
         w_gate, w_up, w_down = in_hbm(w_gate), in_hbm(w_up), in_hbm(w_down)
+        early = lax.ppermute(stage(w_down), ("fs", "pp", "ep"), piece_pairs(lambda p: 1 - p))
         picked = map(in_vmem, pick(hot_ids, w_gate, w_up, w_down))
         *came, late = exchange(hot_ids, w_gate, w_up, w_down, *picked)
-        late = lax.ppermute(late, ("fs", "pp", "ep"), late_pairs())
-        w13, w2, hot13, hot2 = settle(*came)
+        late = lax.ppermute(late, ("fs", "pp", "ep"), piece_pairs(lambda p: p))
+        w13, w2, hot13, hot2 = settle(*came, early)
         w2 = insert(w2, late)
         return w13, w2, hot13, hot2
 

time: 480 us -> 474 us (0.988)
  Pallas kernels: 471 us -> 461 us
    pallas_call x1, Pallas kernels: 430 us -> 422 us  [exchange(): pl.pallas_call(functools.partial(exchange_body, exp_local), out_shape=(pl...]
  transfers between devices with their start and end apart: 1 -> 2, of which waited for: 0 -> 0; matrix products, arithmetic and copies ran while one was open for 0% -> 0% of each run, Pallas kernels for 8% -> 98%
where the time goes in v4:
time: 474 us; the launch traced here: 470 us
  Pallas kernels  461 us (97%)
  starting transfers between devices  8.56 us (2%)
    pallas_call x1, Pallas kernels, exchange(): pl.pallas_call(functools.partial(exchange_body, exp_local), out_shape=(pl...  422 us
    pallas_call x1, Pallas kernels, settle(): pl.pallas_call(functools.partial(settle_body, n_slot, ahead), out_shape=t...  34.1 us
  transfers between devices with their start and end apart: 2, of which 0 were waited for; matrix products, arithmetic and copies ran while one was open for 0% of the time, Pallas kernels for 98%

profile of v4, /device:TPU:0, one launch (start us, length us, event | category | flops | bytes accessed | tf_op | source)
XLA Modules:
  0.0 470.2 jit_solution(2365891856935260986)
XLA Ops:
  0.6 0.0 copy-start
  0.6 1.2 stage.1
  1.8 3.6 collective-permute-start
  5.4 0.0 copy-done
  5.4 3.1 pick.1
  8.5 421.7 %exchange.1 = (bf16[2,3,1024,1024]{3,2,1,0:T(8,128)(2,1)}, bf16[2,3,512,1024]{3,2,1,0:T(8,128)(2,1)}, bf16[2,6,1024,1024]{3,2,1,0:T(8,128)(2,1)}, bf16[2,6,512,1...) custom-call(s32[6]{0:T(128)S(1)} %copy-done, bf16[1,24,1024,128]{3,2,1,0:T(8,128)(2,1)} %gate.3, ...), custom_call_target="tpu_custom_call" | custom-call | flops 68719476736 | bytes 134217728 | tf_op jit(solution)/shard_map/exchange/pallas_call | solution.py:346
  430.2 5.0 %collective-permute-start.1 = (bf16[3,128,1024]{2,1,0:T(8,128)(2,1)}, bf16[3,128,1024]{2,1,0:T(8,128)(2,1)S(1)}, u32[]{:S(2)}, u32[]{:S(2)}) collective-permute-start(bf16[3,128,1024]{2,1,0:T(8,128)(2,1)} %get-tuple-element.24), channel_id=1, source_target_pairs={{0,16},{1,18},{2,20},{3,22},{4,17},{5,19},{6,21},{7,23},{8,24},{9,... | collective-permute-start | bytes 2359304 | tf_op jit(solution)/shard_map/ppermute | solution.py:497
  435.2 0.0 collective-permute-done.early
  435.2 34.1 %settle.1 = (bf16[2,3,1024,1024]{3,2,1,0:T(8,128)(2,1)}, bf16[2,3,512,1024]{3,2,1,0:T(8,128)(2,1)}, bf16[2,6,1024,1024]{3,2,1,0:T(8,128)(2,1)}, bf16[2,6,512,1024]{3,2,1,0:T(8,128)(2,1)}) custom-call(bf16[2,3,1024,1024]{3,2,1,0:T(8,128)(2,1)} %get-tuple-element.19.w13, bf16[2,3,512,1024]{3,2,1,0:T(8,128)(2,1)} %get-tuple-element.20.w2, ...), custom_call_target="tpu_custom_call" | custom-call | flops 905969664 | bytes 113246208 | tf_op jit(solution)/shard_map/settle/pallas_call | solution.py:419
  469.3 0.0 collective-permute-done.1.piece
  469.3 0.9 insert.1
Async XLA Ops:
  0.6 4.8 %copy-start = (s32[6]{0:T(128)S(1)}, s32[6]{0:T(128)}, u32[]{:S(2)}) copy-start(s32[6]{0:T(128)} %ids.3) | copy-start | bytes 76
  1.8 433.4 %collective-permute-start = (bf16[3,128,1024]{2,1,0:T(8,128)(2,1)S(1)}, bf16[3,128,1024]{2,1,0:T(8,128)(2,1)S(1)}, u32[]{:S(2)}, u32[]{:S(2)}) collective-permute-start(bf16[3,128,1024]{2,1,0:T(8,128)(2,1)S(1)} %stage.1), channel_id=1, source_target_pairs={{0,17},{1,19},{2,21},{3,23},{4,16},{5,18},{6,20},{7,22},{8,25},{9,... | collective-permute-start | bytes 2359304 | tf_op jit(solution)/shard_map/ppermute | solution.py:494
  430.2 39.1 %collective-permute-start.1 = (bf16[3,128,1024]{2,1,0:T(8,128)(2,1)}, bf16[3,128,1024]{2,1,0:T(8,128)(2,1)S(1)}, u32[]{:S(2)}, u32[]{:S(2)}) collective-permute-start(bf16[3,128,1024]{2,1,0:T(8,128)(2,1)} %get-tuple-element.24), channel_id=1, source_target_pairs={{0,16},{1,18},{2,20},{3,22},{4,17},{5,19},{6,21},{7,23},{8,24},{9,... | collective-permute-start | bytes 2359304 | tf_op jit(solution)/shard_map/ppermute | solution.py:497

commit v5 on v4

--- a/solution.py
+++ b/solution.py
@@ -16,7 +16,7 @@
 LATE = 2
 OUTER = [(m, b, t) for t in range(N_T) for b in range(2) for m in (1, 3, 2, 0) if (m, t) != (2, 2)]
 INNER = [(m, b, t) for t in range(N_T) for b in range(2) for m in (2, 0, 3, 1) if (m, t) != (3, 2)]
-COUNTS = (4, 0, 0, 0, 24)
+COUNTS = (2, 0, 2, 0, 24)
 
 
 def in_hbm(a):

time: 474 us -> 472 us (level)
  transfers between devices with their start and end apart: 2 -> 2, of which waited for: 0 -> 1; matrix products, arithmetic and copies ran while one was open for 0% -> 0% of each run, Pallas kernels for 98% -> 97%
where the time goes in v5:
time: 472 us; the launch traced here: 471 us
  Pallas kernels  460 us (97%)
  starting transfers between devices  9.86 us (2%)
    pallas_call x1, Pallas kernels, exchange(): pl.pallas_call(functools.partial(exchange_body, exp_local), out_shape=(pl...  420 us
    pallas_call x1, Pallas kernels, settle(): pl.pallas_call(functools.partial(settle_body, n_slot, ahead), out_shape=t...  34.1 us
  transfers between devices with their start and end apart: 2, of which 1 were waited for; matrix products, arithmetic and copies ran while one was open for 0% of the time, Pallas kernels for 97%

profile of v5, /device:TPU:0, one launch (start us, length us, event | category | flops | bytes accessed | tf_op | source)
XLA Modules:
  0.0 470.7 jit_solution(4128006191959595120)
XLA Ops:
  0.6 0.0 copy-start
  0.6 1.2 stage.1
  1.8 3.6 collective-permute-start
  5.4 0.0 copy-done
  5.4 3.3 pick.1
  8.7 420.3 %exchange.1 = (bf16[2,3,1024,1024]{3,2,1,0:T(8,128)(2,1)}, bf16[2,3,512,1024]{3,2,1,0:T(8,128)(2,1)}, bf16[2,6,1024,1024]{3,2,1,0:T(8,128)(2,1)}, bf16[2,6,512,1...) custom-call(s32[6]{0:T(128)S(1)} %copy-done, bf16[1,24,1024,128]{3,2,1,0:T(8,128)(2,1)} %gate.3, ...), custom_call_target="tpu_custom_call" | custom-call | flops 68719476736 | bytes 134217728 | tf_op jit(solution)/shard_map/exchange/pallas_call | solution.py:346
  429.0 6.3 %collective-permute-start.1 = (bf16[3,128,1024]{2,1,0:T(8,128)(2,1)}, bf16[3,128,1024]{2,1,0:T(8,128)(2,1)S(1)}, u32[]{:S(2)}, u32[]{:S(2)}) collective-permute-start(bf16[3,128,1024]{2,1,0:T(8,128)(2,1)} %get-tuple-element.24), channel_id=1, source_target_pairs={{0,16},{1,18},{2,20},{3,22},{4,17},{5,19},{6,21},{7,23},{8,24},{9,... | collective-permute-start | bytes 2359304 | tf_op jit(solution)/shard_map/ppermute | solution.py:497
  435.3 0.0 collective-permute-done.early
  435.3 34.1 %settle.1 = (bf16[2,3,1024,1024]{3,2,1,0:T(8,128)(2,1)}, bf16[2,3,512,1024]{3,2,1,0:T(8,128)(2,1)}, bf16[2,6,1024,1024]{3,2,1,0:T(8,128)(2,1)}, bf16[2,6,512,1024]{3,2,1,0:T(8,128)(2,1)}) custom-call(bf16[2,3,1024,1024]{3,2,1,0:T(8,128)(2,1)} %get-tuple-element.19.w13, bf16[2,3,512,1024]{3,2,1,0:T(8,128)(2,1)} %get-tuple-element.20.w2, ...), custom_call_target="tpu_custom_call" | custom-call | flops 905969664 | bytes 113246208 | tf_op jit(solution)/shard_map/settle/pallas_call | solution.py:419
  469.4 0.4 collective-permute-done.1.piece
  469.8 0.9 insert.1
Async XLA Ops:
  0.6 4.8 %copy-start = (s32[6]{0:T(128)S(1)}, s32[6]{0:T(128)}, u32[]{:S(2)}) copy-start(s32[6]{0:T(128)} %ids.3) | copy-start | bytes 76
  1.8 433.5 %collective-permute-start = (bf16[3,128,1024]{2,1,0:T(8,128)(2,1)S(1)}, bf16[3,128,1024]{2,1,0:T(8,128)(2,1)S(1)}, u32[]{:S(2)}, u32[]{:S(2)}) collective-permute-start(bf16[3,128,1024]{2,1,0:T(8,128)(2,1)S(1)} %stage.1), channel_id=1, source_target_pairs={{0,17},{1,19},{2,21},{3,23},{4,16},{5,18},{6,20},{7,22},{8,25},{9,... | collective-permute-start | bytes 2359304 | tf_op jit(solution)/shard_map/ppermute | solution.py:494
  429.0 40.8 %collective-permute-start.1 = (bf16[3,128,1024]{2,1,0:T(8,128)(2,1)}, bf16[3,128,1024]{2,1,0:T(8,128)(2,1)S(1)}, u32[]{:S(2)}, u32[]{:S(2)}) collective-permute-start(bf16[3,128,1024]{2,1,0:T(8,128)(2,1)} %get-tuple-element.24), channel_id=1, source_target_pairs={{0,16},{1,18},{2,20},{3,22},{4,17},{5,19},{6,21},{7,23},{8,24},{9,... | collective-permute-start | bytes 2359304 | tf_op jit(solution)/shard_map/ppermute | solution.py:497
